TPU v7x, 32 devices: a whole 2x2x4 slice. The times are simulated.
32 devices in a mesh: groups: 2 (over y), src: 4 (over z), tgt: 2 (over x), ill: 2 (over core).
Axes of the slice: x: 2, y: 2, z: 4, core: 2. Of those that a mesh axis runs over, the one named last changes fastest.
Arguments:
- coeffs: bfloat16 [2, 64, 8, 8, 512], P(None, ('groups', 'ill'), 'src', 'tgt'), parts along dimension 1, may hold values from -6 to 6
- reflection: float32 [2, 16, 8, 512], P(None, ('groups', 'src'), 'tgt'), parts along dimension 1, may hold values from -4.2 to 4.2
- interp: float32 [2, 3, 2, 2, 3, 8, 8], replicated, may hold values from -1 to 1
- orders: int32 [512], replicated, may hold values from 0 to 511, each once
Outputs:
- far_field: bfloat16 [2, 64, 8, 8, 512], P(None, ('groups', 'ill'), 'src', 'tgt'), parts along dimension 1
There are 2 independent parts, one for each index of `groups`. A program takes and returns all parts, laid end to end along the dimension named above; an argument that names none is the same for every part. Nothing has to cross between parts.
Inputs may be any that keep to these rules, and one draw needn't show every extreme that they name: `orders`: each number below 512 appears exactly once.
All inputs are finite; a program needn't handle non-finite values.
Results may differ from a plain program's by a relative error of at most 0.028.
Values may be sent and summed in bfloat16 or wider, within the bound.
No kernel may reach another device: no remote copies, remote signals or barrier semaphores. Data moves between devices by JAX's collectives and lax.ppermute only.
A program may use at most 64 MiB of HBM per device.

v0:
```python
import functools
import math

import jax
import jax.numpy as jnp
from jax import lax
from jax.experimental import pallas as pl
from jax.experimental.pallas import tpu as pltpu
from jax.sharding import PartitionSpec as P


PHASE_RATE = 0.3
ALONG_SECOND = 1.7
DIRECTIONS = ((0.6, 0.48, 0.64), (-0.36, 0.8, 0.48))
F32 = jnp.float32
BF16 = jnp.bfloat16
CHUNKS = 2
LANES = 128
EARLY = 4


def partner_2(value, axis, bit):
    mask = 2**bit
    pairs = [(source, source ^ mask) for source in range(lax.axis_size(axis))]
    return lax.ppermute(value, axis, pairs)


def node_value(digits, order_count):
    return jnp.cos(math.pi * (2.0 * digits.astype(F32) + 1.0) / (2.0 * order_count))


def plan_levels(level_count, extents, locals_):
    levels = []
    for operator in range(2):
        top = extents[operator].bit_length() - 2
        local_bits = locals_[operator].bit_length() - 1
        for level in range(level_count):
            bit = top - level
            if bit >= local_bits:
                levels.append((operator, level, ("src", "tgt")[operator], bit - local_bits))
            else:
                levels.append((operator, level, None, bit))
    return levels


def table_body(levels, boxes_shape, first_other, order_count, orders_ref, reflection_ref, table_ref):
    boxes_u, boxes_v = boxes_shape
    boxes = boxes_u * boxes_v
    coef_count = orders_ref.shape[1]
    orders = orders_ref[...]
    digits = (orders // (order_count * order_count), orders // order_count % order_count, orders % order_count)
    row = lax.broadcasted_iota(jnp.int32, (boxes, coef_count), 0)
    picked = jnp.where(row == 0, digits[0], jnp.where(row == 1, digits[1], digits[2]))
    values = node_value(picked, order_count)
    u = (row // boxes_v).astype(F32)
    v = (row % boxes_v).astype(F32)
    src = lax.axis_index("src")
    tgt = lax.axis_index("tgt")

    def corner(src_index):
        first = (src_index * boxes_u).astype(F32) + u + 0.5
        return first + ALONG_SECOND * ((tgt * boxes_v).astype(F32) + v + 0.5)

    def times(a, b):
        return a[0] * b[0] - a[1] * b[1], a[0] * b[1] + a[1] * b[0]

    def rounded(a):
        return a[0].astype(BF16).astype(F32), a[1].astype(BF16).astype(F32)

    def put(index, value):
        table_ref[index, 0] = value[0]
        table_ref[index, 1] = value[1]

    for operator in range(2):
        direction = DIRECTIONS[operator]
        products = direction[0] * values[0:1] + direction[1] * values[1:2] + direction[2] * values[2:3]
        angle = PHASE_RATE * corner(src) * products
        base = (jnp.cos(angle), jnp.sin(angle))
        power = base
        mine = [i for i, level in enumerate(levels) if level[0] == operator]
        for number, index in enumerate(mine):
            if number:
                power = times(power, base)
            phase = rounded(power)
            if operator == 1 and number == 0:
                weight = [
                    jnp.concatenate([reflection_ref[part, i] for i in range(boxes_u)], axis=0) for part in range(2)
                ]
                phase = times(phase, weight)
            put(index, phase)
        if operator == 0:
            angle = PHASE_RATE * corner(src ^ first_other) * products
            put(len(levels), rounded((jnp.cos(angle), jnp.sin(angle))))


def spread_body(interp_ref, spread_ref):
    order_count = interp_ref.shape[-1]
    coef_count = spread_ref.shape[-1]
    column = lax.broadcasted_iota(jnp.int32, (order_count, coef_count), 1)
    point = lax.broadcasted_iota(jnp.int32, (order_count, coef_count), 0)
    column_digits = (column // (order_count * order_count), column // order_count % order_count, column % order_count)
    for d in range(3):
        chosen = (column_digits[d] == point).astype(BF16)
        value = jnp.swapaxes(interp_ref[:, d], 1, 2).reshape(-1, order_count)
        high = value.astype(BF16)
        rest = value - high.astype(F32)
        middle = rest.astype(BF16)
        low = (rest - middle.astype(F32)).astype(BF16)
        spread_ref[d] = dot(high, chosen) + (dot(middle, chosen) + dot(low, chosen))


def build_body(base, axis, bit, count, spread_ref, *w_refs):
    order_count = round(w_refs[0].shape[1] ** (1 / 3))
    square = order_count * order_count
    if axis is None:
        which = [base + i for i in range(count)]
    else:
        own = lax.axis_index(axis) >> bit & 1
        which = [base + 3 * own, base + own + 1]
    for number in range(count):
        begin = which[number] * order_count
        if axis is not None:
            begin = pl.multiple_of(begin, order_count)
        first, second, third = [spread_ref[d, pl.ds(begin, order_count)] for d in range(3)]
        w_ref = w_refs[number]
        for x in range(order_count):
            lead = first[x : x + 1] * second
            for y in range(0, order_count, 2):
                block = jnp.concatenate([lead[y : y + 1] * third, lead[y + 1 : y + 2] * third])
                w_ref[x * square + y * order_count : x * square + (y + 2) * order_count] = block.astype(BF16)


def modulate(src, table, index, dst, boxes, ill, place):
    half = boxes * ill
    for box in range(boxes):
        real = src[box * ill : (box + 1) * ill].astype(F32)
        imag = src[half + box * ill : half + (box + 1) * ill].astype(F32)
        cos = table[index, 0, box : box + 1]
        sin = table[index, 1, box : box + 1]
        dst[place(0, box)] = (cos * real - sin * imag).astype(BF16)
        dst[place(1, box)] = (cos * imag + sin * real).astype(BF16)


def strided(flat_ref, start, count, stride):
    return jnp.concatenate(
        [flat_ref[t, pl.ds(start, count, stride=stride)] for t in range(flat_ref.shape[0])], axis=1
    )


def modulate_raw(x_ref, table, index, flat_ref, dst):
    _, ill, boxes_u, boxes_v, _ = x_ref.shape
    boxes = boxes_u * boxes_v
    half = boxes * ill
    for part in range(2):
        for i in range(ill):
            for u in range(boxes_u):
                piece = x_ref[part, i, u].astype(F32)
                for t in range(flat_ref.shape[0]):
                    flat_ref[t, pl.ds(part * half + i * boxes + u * boxes_v, boxes_v)] = piece[:, t * LANES : (t + 1) * LANES]
    for box in range(boxes):
        real = strided(flat_ref, box, ill, boxes)
        imag = strided(flat_ref, half + box, ill, boxes)
        cos = table[index, 0, box : box + 1]
        sin = table[index, 1, box : box + 1]
        dst[box * ill : (box + 1) * ill] = (cos * real - sin * imag).astype(BF16)
        dst[half + box * ill : half + (box + 1) * ill] = (cos * imag + sin * real).astype(BF16)


def straight(boxes, ill):
    half = boxes * ill
    return lambda part, box: pl.ds(part * half + box * ill, ill)


def dot(a, b):
    return jnp.dot(a, b, preferred_element_type=F32)


def piece_body(begin, x_ref, *refs):
    out_ref, sem = refs[-2:]
    copy = pltpu.make_async_copy(x_ref.at[:, pl.ds(begin, out_ref.shape[1])], out_ref, sem)
    copy.start()
    copy.wait()


def own_body(index, raw, x_ref, table_ref, w_ref, out_ref, flat_ref, mod_ref):
    if raw:
        modulate_raw(x_ref, table_ref, index, flat_ref, mod_ref)
        out_ref[...] = dot(mod_ref[...], w_ref[...])
    else:
        out_ref[...] = dot(x_ref[...], w_ref[...])


def rest_body(shape, partner_index, pairs, send_index, begin, done, *refs):
    boxes_u, boxes_v, ill = shape
    boxes = boxes_u * boxes_v
    half = boxes * ill
    part_ref, got_ref, table_ref, w_ref = refs[:4]
    pair_refs = refs[4 : 4 + 4 * len(pairs)]
    if send_index is None:
        if done is None:
            turned_ref, state_ref, mod_ref, flat_ref = refs[-4:]
        else:
            out_ref, state_ref, mod_ref, flat_ref, turned_ref, sem = refs[-6:]
            copies = []
            for number in range(done):
                earlier = refs[4 + 4 * len(pairs) + number]
                place = pl.ds(number * ill, ill)
                copies.append(pltpu.make_async_copy(earlier, out_ref.at[:, place], sem.at[number]))
                copies[-1].start()
    else:
        out_ref, state_ref, mod_ref, flat_ref = refs[-4:]
    if partner_index is None:
        got = got_ref[...]
    else:
        modulate_raw(got_ref, table_ref, partner_index, flat_ref, mod_ref)
        got = mod_ref[...]
    state_ref[...] = part_ref[...] + dot(got, w_ref[...])
    for number, (index, operator, bit) in enumerate(pairs):
        w4 = pair_refs[4 * number : 4 * number + 4]
        box_bit = bit + (boxes_v.bit_length() - 1 if operator == 0 else 0)
        low_mask = (1 << box_bit) - 1

        def place(part, box):
            side = box >> box_bit & 1
            rank = (box >> (box_bit + 1) << box_bit) | (box & low_mask)
            return pl.ds(side * half + part * (half // 2) + rank * ill, ill)

        modulate(state_ref, table_ref, index, mod_ref, boxes, ill, place)
        for side in range(2):
            result = dot(mod_ref[:half], w4[2 * side][...]) + dot(mod_ref[half:], w4[2 * side + 1][...])
            for part in range(2):
                for box in range(boxes):
                    if box >> box_bit & 1 == side:
                        start = place(part, box).start - side * half
                        state_ref[straight(boxes, ill)(part, box)] = result[start : start + ill]
    if send_index is not None:
        modulate(state_ref, table_ref, send_index, out_ref, boxes, ill, straight(boxes, ill))
        return
    tiles = flat_ref.shape[0]
    for part in range(2):
        for box in range(boxes):
            value = state_ref[straight(boxes, ill)(part, box)]
            for t in range(tiles):
                flat_ref[t, pl.ds(part * half + box, ill, stride=boxes)] = value[:, t * LANES : (t + 1) * LANES]
        for i in range(ill):
            for u in range(boxes_u):
                place = pl.ds(part * half + i * boxes + u * boxes_v, boxes_v)
                turned_ref[part, i, u] = jnp.concatenate([flat_ref[t, place] for t in range(tiles)], axis=1).astype(BF16)
        if done is not None:
            target = out_ref.at[part, pl.ds(begin, ill)]
            copies.append(pltpu.make_async_copy(turned_ref.at[part], target, sem.at[done + part]))
            copies[-1].start()
    if done is not None:
        for copy in copies:
            copy.wait()


def call(body, outs, scratch, flops, moved, *args, in_specs=None, out_specs=None, aliases=None, limit=6 * 1024 * 1024):
    vmem = pl.BlockSpec(memory_space=pltpu.VMEM)
    many = isinstance(outs, (tuple, list))
    return pl.pallas_call(
        body,
        out_shape=outs,
        in_specs=in_specs or [vmem] * len(args),
        out_specs=out_specs or ([vmem] * len(outs) if many else vmem),
        scratch_shapes=scratch,
        input_output_aliases=aliases or {},
        compiler_params=pltpu.CompilerParams(vmem_limit_bytes=limit),
        cost_estimate=pl.CostEstimate(flops=flops, bytes_accessed=moved, transcendentals=0),
    )(*args)


def on_device(coeffs, reflection, interp, orders):
    level_count = interp.shape[1]
    order_count = interp.shape[-1]
    _, ill, boxes_u, boxes_v, coef_count = coeffs.shape
    boxes = boxes_u * boxes_v
    extents = (boxes_u * lax.axis_size("src"), boxes_v * lax.axis_size("tgt"))
    levels = plan_levels(level_count, extents, (boxes_u, boxes_v))
    assert levels[0][2] == "src"
    swaps = [i for i, level in enumerate(levels) if level[2] is not None]
    vmem = pl.BlockSpec(memory_space=pltpu.VMEM)
    anywhere = pl.BlockSpec(memory_space=pl.ANY)

    chunk = ill // CHUNKS if ill % CHUNKS == 0 else ill
    rows = 2 * boxes * chunk
    begins = list(range(0, ill, chunk))
    piece_shape = (2, chunk, boxes_u, boxes_v, coef_count)

    def piece(begin, after):
        return call(
            functools.partial(piece_body, begin),
            jax.ShapeDtypeStruct(piece_shape, BF16),
            [pltpu.SemaphoreType.DMA],
            1000,
            rows * coef_count * 4,
            coeffs,
            *after,
            in_specs=[anywhere] * (1 + len(after)),
            limit=6 * 1024 * 1024,
        )

    pieces = [coeffs[:, :chunk]]

    factors = interp.reshape(-1, 3, order_count, order_count)
    spread = call(
        spread_body,
        jax.ShapeDtypeStruct((3, factors.shape[0] * order_count, coef_count), F32),
        [],
        2000000,
        1000000,
        factors,
    )
    table = call(
        functools.partial(table_body, levels, (boxes_u, boxes_v), 2 ** levels[0][3], order_count),
        jax.ShapeDtypeStruct((len(levels) + 1, 2, boxes, coef_count), F32),
        [],
        2000000,
        1000000,
        orders.reshape(1, coef_count),
        reflection,
    )
    matrices = []
    for operator, level, axis, bit in levels:
        count = 4 if axis is None else 2
        matrices.append(
            call(
                functools.partial(build_body, (operator * level_count + level) * 4, axis, bit, count),
                [jax.ShapeDtypeStruct((coef_count, coef_count), BF16)] * count,
                [],
                count * 20000000,
                count * 2 * coef_count * coef_count,
                spread,
            )
        )

    for begin in begins[1:]:
        pieces.append(piece(begin, [table] + [w[1] for w in matrices[:EARLY]]))
    raws = []
    for value in pieces:
        raws.append(partner_2(value, levels[0][2], levels[0][3]))

    product_flops = 2 * rows * coef_count * coef_count

    def own_part(number, current):
        index = swaps[number]
        return call(
            functools.partial(own_body, index, number == 0),
            jax.ShapeDtypeStruct((rows, coef_count), F32),
            [pltpu.VMEM((coef_count // LANES, rows, LANES), F32), pltpu.VMEM((rows, coef_count), BF16)],
            product_flops,
            rows * coef_count * 6 + coef_count * coef_count * 2,
            current,
            table,
            matrices[index][0],
        )

    def rest_part(number, own, partner, begin, earlier):
        index = swaps[number]
        last = number + 1 == len(swaps)
        after = len(levels) if last else swaps[number + 1]
        pairs = [(i, levels[i][0], levels[i][3]) for i in range(index + 1, after)]
        args = [own, partner, table, matrices[index][1]]
        for i, _, _ in pairs:
            args += matrices[i]
        specs = [vmem] * len(args)
        scratch = [
            pltpu.VMEM((rows, coef_count), F32),
            pltpu.VMEM((rows, coef_count), BF16),
            pltpu.VMEM((coef_count // LANES, rows, LANES), F32),
        ]
        out = jax.ShapeDtypeStruct((rows, coef_count), BF16)
        out_specs, done = vmem, None
        if last and begin < begins[-1]:
            out = jax.ShapeDtypeStruct(piece_shape, BF16)
        elif last:
            out = jax.ShapeDtypeStruct(coeffs.shape, BF16)
            out_specs, done = anywhere, len(earlier)
            scratch += [pltpu.VMEM(piece_shape, BF16), pltpu.SemaphoreType.DMA((len(begins) + 1,))]
            args += earlier
            specs += [vmem] * len(earlier)
        return call(
            functools.partial(
                rest_body,
                (boxes_u, boxes_v, chunk),
                len(levels) if number == 0 else None,
                pairs,
                None if last else after,
                begin,
                done,
            ),
            out,
            scratch,
            product_flops * (1 + 2 * len(pairs)),
            rows * coef_count * 8 + coef_count * coef_count * 2 * (1 + 4 * len(pairs)),
            *args,
            in_specs=specs,
            out_specs=out_specs,
        )

    currents, gots = pieces, raws
    for number, index in enumerate(swaps):
        if number:
            gots = []
            for current in currents:
                gots.append(partner_2(current, levels[index][2], levels[index][3]))
        owns = [own_part(number, current) for current in currents]
        following = []
        for own, got, begin in zip(owns, gots, begins):
            following.append(rest_part(number, own, got, begin, following))
        currents = following
    return currents[-1]


def solution(mesh):
    in_specs = (
        P(None, ("groups", "ill"), "src", "tgt", None),
        P(None, ("groups", "src"), "tgt", None),
        P(),
        P(),
    )
    out_specs = P(None, ("groups", "ill"), "src", "tgt", None)

    return jax.shard_map(on_device, mesh=mesh, in_specs=in_specs, out_specs=out_specs, check_vma=False)
```

profile of v0, /device:TPU:0, one launch (start us, length us, event | category | flops | bytes accessed | tf_op | source)
XLA Modules:
  0.0 30.9 jit_solution(18136955314885326689)
XLA Ops:
  0.0 1.0 %slice.3.x_ref = bf16[2,8,2,4,512]{4,3,2,1,0:T(4,128)(2,1)S(1)} slice(bf16[2,16,2,4,512]{4,3,2,1,0:T(4,128)(2,1)} %x_ref.1), slice={[0:2], [0:8], [0:2], [0:4], [0:512]} | slice | bytes 262144 | tf_op jit(solution)/shard_map/slice | solution.py:303
  1.0 4.1 %collective-permute-start.3 = (bf16[2,8,2,4,512]{4,3,2,1,0:T(4,128)(2,1)S(1)}, bf16[2,8,2,4,512]{4,3,2,1,0:T(4,128)(2,1)S(1)}, u32[]{:S(2)}, u32[]{:S(2)}) collective-permute-start(bf16[2,8,2,4,512]{4,3,2,1,0:T(4,128)(2,1)S(1)} %slice.3.x_ref), channel_id=1, source_target_pairs={{0,8},{4,12},{8,0},{12,4},{1,9},{5,13},{9,1},{13,5},{2,10},{6,14},... | collective-permute-start | bytes 393224 | tf_op jit(solution)/shard_map/ppermute | solution.py:25
  5.1 1.0 %copy-done.1 = f32[2,3,2,2,3,8,8]{6,5,4,3,2,1,0:T(8,128)S(1)} copy-done((f32[2,3,2,2,3,8,8]{6,5,4,3,2,1,0:T(8,128)S(1)}, f32[2,3,2,2,3,8,8]{6,5,4,3,2,1,0:T(8,128)}, u32[]{:S(2)}) %copy-start.1) | copy-done | bytes 18456
  6.1 0.7 %shard_map.47.spread_ref = f32[3,192,512]{2,1,0:T(8,128)S(1)} custom-call(f32[24,3,8,8]{3,2,1,0:T(8,128)S(1)} %bitcast.2), custom_call_target="tpu_custom_call" | custom-call | flops 2000000 | bytes 1000000 | tf_op jit(solution)/shard_map/pallas_call | solution.py:261
  6.8 0.3 shard_map.46.refs_0_.table_ref.refs_2_
  7.7 0.4 %shard_map.50 = (bf16[512,512]{1,0:T(8,128)(2,1)S(1)}, bf16[512,512]{1,0:T(8,128)(2,1)S(1)}, bf16[512,512]{1,0:T(8,128)(2,1)S(1)}, bf16[512,512]{1,0:T(8,128)(2,1)S(1)}) custom-call(f32[3,192,512]{2,1,0:T(8,128)S(1)} %shard_map.47.spread_ref), custom_call_target="tpu_custom_call" | custom-call | flops 80000000 | bytes 2097152 | tf_op jit(solution)/shard_map/pallas_call | solution.py:261
  8.1 0.4 %copy-done = bf16[2,16,2,4,512]{4,3,2,1,0:T(4,128)(2,1)S(1)} copy-done((bf16[2,16,2,4,512]{4,3,2,1,0:T(4,128)(2,1)S(1)}, bf16[2,16,2,4,512]{4,3,2,1,0:T(4,128)(2,1)}, u32[]{:S(2)}) %copy-start) | copy-done | bytes 262168
  8.9 2.5 %collective-permute-done.3.refs_1_ = bf16[2,8,2,4,512]{4,3,2,1,0:T(4,128)(2,1)S(1)} collective-permute-done((bf16[2,8,2,4,512]{4,3,2,1,0:T(4,128)(2,1)S(1)}, bf16[2,8,2,4,512]{4,3,2,1,0:T(4,128)(2,1)S(1)}, u32[]{:S(2)}, u32[]{:S(2)}) %collective-permute-start.3) | collective-permute-done | bytes 131104 | tf_op jit(solution)/shard_map/ppermute | solution.py:25
  11.4 0.3 shard_map.61.x_ref
  11.7 3.7 %collective-permute-start.4 = (bf16[128,512]{1,0:T(8,128)(2,1)S(1)}, bf16[128,512]{1,0:T(8,128)(2,1)S(1)}, u32[]{:S(2)}, u32[]{:S(2)}) collective-permute-start(bf16[128,512]{1,0:T(8,128)(2,1)S(1)} %shard_map.61.x_ref), channel_id=1, source_target_pairs={{0,4},{4,0},{8,12},{12,8},{1,5},{5,1},{9,13},{13,9},{2,6},{6,2},{1... | collective-permute-start | bytes 393224 | tf_op jit(solution)/shard_map/ppermute | solution.py:25
  15.7 1.7 %collective-permute-done.refs_1_ = bf16[2,8,2,4,512]{4,3,2,1,0:T(4,128)(2,1)S(1)} collective-permute-done((bf16[2,8,2,4,512]{4,3,2,1,0:T(4,128)(2,1)S(1)}, bf16[2,8,2,4,512]{4,3,2,1,0:T(4,128)(2,1)S(1)}, u32[]{:S(2)}, u32[]{:S(2)}) %collective-permute-start) | collective-permute-done | bytes 131104 | tf_op jit(solution)/shard_map/ppermute | solution.py:25
  17.3 0.3 shard_map.54.x_ref
  17.6 0.5 %collective-permute-start.1 = (bf16[128,512]{1,0:T(8,128)(2,1)S(1)}, bf16[128,512]{1,0:T(8,128)(2,1)S(1)}, u32[]{:S(2)}, u32[]{:S(2)}) collective-permute-start(bf16[128,512]{1,0:T(8,128)(2,1)S(1)} %shard_map.54.x_ref), channel_id=1, source_target_pairs={{0,4},{4,0},{8,12},{12,8},{1,5},{5,1},{9,13},{13,9},{2,6},{6,2},{1... | collective-permute-start | bytes 393224 | tf_op jit(solution)/shard_map/ppermute | solution.py:25
  18.3 1.8 %collective-permute-done.4.refs_1_ = bf16[128,512]{1,0:T(8,128)(2,1)S(1)} collective-permute-done((bf16[128,512]{1,0:T(8,128)(2,1)S(1)}, bf16[128,512]{1,0:T(8,128)(2,1)S(1)}, u32[]{:S(2)}, u32[]{:S(2)}) %collective-permute-start.4) | collective-permute-done | bytes 131104 | tf_op jit(solution)/shard_map/ppermute | solution.py:25
  20.1 0.7 %shard_map.63.x_ref = bf16[128,512]{1,0:T(8,128)(2,1)S(1)} custom-call(f32[128,512]{1,0:T(8,128)S(1)} %shard_map.62.refs_0_, bf16[128,512]{1,0:T(8,128)(2,1)S(1)} %collective-permute-done.4.refs_1_, f32[7,2,8,512]{3,2,1,0:T(8,128)S(1)} %shard_map.46.refs_0_.table_ref.refs_2_, bf16[512,512]{1,0:T(8,128)(2,1)S(1)} %get-tuple-element.24.refs_2_.refs_3_, ...), custom_call_target="tpu_custom_call" | custom-call | flops 201326592 | bytes 3145728 | tf_op jit(solution)/shard_map/pallas_call | solution.py:261
  20.8 1.6 %collective-permute-start.5 = (bf16[128,512]{1,0:T(8,128)(2,1)S(1)}, bf16[128,512]{1,0:T(8,128)(2,1)S(1)}, u32[]{:S(2)}, u32[]{:S(2)}) collective-permute-start(bf16[128,512]{1,0:T(8,128)(2,1)S(1)} %shard_map.63.x_ref), channel_id=1, source_target_pairs={{0,2},{2,0},{1,3},{3,1},{4,6},{6,4},{5,7},{7,5},{8,10},{10,8},{9,1... | collective-permute-start | bytes 393224 | tf_op jit(solution)/shard_map/ppermute | solution.py:25
  22.9 0.7 %shard_map.56.x_ref = bf16[128,512]{1,0:T(8,128)(2,1)S(1)} custom-call(f32[128,512]{1,0:T(8,128)S(1)} %shard_map.55.refs_0_, bf16[128,512]{1,0:T(8,128)(2,1)S(1)} %collective-permute-done.1.refs_1_, f32[7,2,8,512]{3,2,1,0:T(8,128)S(1)} %shard_map.46.refs_0_.table_ref.refs_2_, bf16[512,512]{1,0:T(8,128)(2,1)S(1)} %get-tuple-element.24.refs_2_.refs_3_, ...), custom_call_target="tpu_custom_call" | custom-call | flops 201326592 | bytes 3145728 | tf_op jit(solution)/shard_map/pallas_call | solution.py:261
  23.6 1.6 %collective-permute-start.2 = (bf16[128,512]{1,0:T(8,128)(2,1)S(1)}, bf16[128,512]{1,0:T(8,128)(2,1)S(1)}, u32[]{:S(2)}, u32[]{:S(2)}) collective-permute-start(bf16[128,512]{1,0:T(8,128)(2,1)S(1)} %shard_map.56.x_ref), channel_id=1, source_target_pairs={{0,2},{2,0},{1,3},{3,1},{4,6},{6,4},{5,7},{7,5},{8,10},{10,8},{9,1... | collective-permute-start | bytes 393224 | tf_op jit(solution)/shard_map/ppermute | solution.py:25
  25.1 0.4 %shard_map.59 = (bf16[512,512]{1,0:T(8,128)(2,1)S(1)}, bf16[512,512]{1,0:T(8,128)(2,1)S(1)}, bf16[512,512]{1,0:T(8,128)(2,1)S(1)}, bf16[512,512]{1,0:T(8,128)(2,1)S(1)}) custom-call(f32[3,192,512]{2,1,0:T(8,128)S(1)} %shard_map.47.spread_ref), custom_call_target="tpu_custom_call" | custom-call | flops 80000000 | bytes 2097152 | tf_op jit(solution)/shard_map/pallas_call | solution.py:261
  25.5 0.4 %shard_map.58 = (bf16[512,512]{1,0:T(8,128)(2,1)S(1)}, bf16[512,512]{1,0:T(8,128)(2,1)S(1)}, bf16[512,512]{1,0:T(8,128)(2,1)S(1)}, bf16[512,512]{1,0:T(8,128)(2,1)S(1)}) custom-call(f32[3,192,512]{2,1,0:T(8,128)S(1)} %shard_map.47.spread_ref), custom_call_target="tpu_custom_call" | custom-call | flops 80000000 | bytes 2097152 | tf_op jit(solution)/shard_map/pallas_call | solution.py:261
  26.3 0.5 %collective-permute-done.5.refs_1_ = bf16[128,512]{1,0:T(8,128)(2,1)S(1)} collective-permute-done((bf16[128,512]{1,0:T(8,128)(2,1)S(1)}, bf16[128,512]{1,0:T(8,128)(2,1)S(1)}, u32[]{:S(2)}, u32[]{:S(2)}) %collective-permute-start.5) | collective-permute-done | bytes 131104 | tf_op jit(solution)/shard_map/ppermute | solution.py:25
  26.9 1.2 %shard_map.65.refs_12_ = bf16[2,8,2,4,512]{4,3,2,1,0:T(4,128)(2,1)S(1)} custom-call(f32[128,512]{1,0:T(8,128)S(1)} %shard_map.64.refs_0_, bf16[128,512]{1,0:T(8,128)(2,1)S(1)} %collective-permute-done.5.refs_1_, f32[7,2,8,512]{3,2,1,0:T(8,128)S(1)} %shard_map.46.refs_0_.table_ref.refs_2_, bf16[512,512]{1,0:T(8,128)(2,1)S(1)} %get-tuple-element.26.refs_4_.refs_3_, ...), custom_call_target="tpu_custom_call" | custom-call | flops 335544320 | bytes 5242880 | tf_op jit(solution)/shard_map/pallas_call | solution.py:261
  28.0 1.0 %collective-permute-done.2.refs_1_ = bf16[128,512]{1,0:T(8,128)(2,1)S(1)} collective-permute-done((bf16[128,512]{1,0:T(8,128)(2,1)S(1)}, bf16[128,512]{1,0:T(8,128)(2,1)S(1)}, u32[]{:S(2)}, u32[]{:S(2)}) %collective-permute-start.2) | collective-permute-done | bytes 131104 | tf_op jit(solution)/shard_map/ppermute | solution.py:25
  29.1 1.8 %shard_map.66 = bf16[2,16,2,4,512]{4,3,2,1,0:T(4,128)(2,1)} custom-call(f32[128,512]{1,0:T(8,128)S(1)} %shard_map.57.refs_0_, bf16[128,512]{1,0:T(8,128)(2,1)S(1)} %collective-permute-done.2.refs_1_, f32[7,2,8,512]{3,2,1,0:T(8,128)S(1)} %shard_map.46.refs_0_.table_ref.refs_2_, bf16[512,512]{1,0:T(8,128)(2,1)S(1)} %get-tuple-element.26.refs_4_.refs_3_, ...), custom_call_target="tpu_custom_call" | custom-call | flops 335544320 | bytes 5242880 | tf_op jit(solution)/shard_map/pallas_call | solution.py:261
  (18 shorter events, 2.5 us)
Async XLA Ops:
  0.0 6.7 %copy-start.3 = (s32[512]{0:T(512)S(1)}, s32[512]{0:T(512)}, u32[]{:S(2)}) copy-start(s32[512]{0:T(512)} %param.7) | copy-start | bytes 6148
  0.0 6.7 %copy-start.2 = (f32[2,2,4,512]{3,2,1,0:T(4,128)S(1)}, f32[2,2,4,512]{3,2,1,0:T(4,128)}, u32[]{:S(2)}) copy-start(f32[2,2,4,512]{3,2,1,0:T(4,128)} %reflection_ref.1) | copy-start | bytes 98308
  1.0 10.4 %collective-permute-start.3 = (bf16[2,8,2,4,512]{4,3,2,1,0:T(4,128)(2,1)S(1)}, bf16[2,8,2,4,512]{4,3,2,1,0:T(4,128)(2,1)S(1)}, u32[]{:S(2)}, u32[]{:S(2)}) collective-permute-start(bf16[2,8,2,4,512]{4,3,2,1,0:T(4,128)(2,1)S(1)} %slice.3.x_ref), channel_id=1, source_target_pairs={{0,8},{4,12},{8,0},{12,4},{1,9},{5,13},{9,1},{13,5},{2,10},{6,14},... | collective-permute-start | bytes 393224 | tf_op jit(solution)/shard_map/ppermute | solution.py:25
  5.1 1.0 %copy-start.1 = (f32[2,3,2,2,3,8,8]{6,5,4,3,2,1,0:T(8,128)S(1)}, f32[2,3,2,2,3,8,8]{6,5,4,3,2,1,0:T(8,128)}, u32[]{:S(2)}) copy-start(f32[2,3,2,2,3,8,8]{6,5,4,3,2,1,0:T(8,128)} %param.6) | copy-start | bytes 55300
  7.5 1.0 %copy-start = (bf16[2,16,2,4,512]{4,3,2,1,0:T(4,128)(2,1)S(1)}, bf16[2,16,2,4,512]{4,3,2,1,0:T(4,128)(2,1)}, u32[]{:S(2)}) copy-start(bf16[2,16,2,4,512]{4,3,2,1,0:T(4,128)(2,1)} %x_ref.1) | copy-start | bytes 786436
  8.5 8.8 %collective-permute-start = (bf16[2,8,2,4,512]{4,3,2,1,0:T(4,128)(2,1)S(1)}, bf16[2,8,2,4,512]{4,3,2,1,0:T(4,128)(2,1)S(1)}, u32[]{:S(2)}, u32[]{:S(2)}) collective-permute-start(bf16[2,8,2,4,512]{4,3,2,1,0:T(4,128)(2,1)S(1)} %shard_map.52.x_ref), channel_id=1, source_target_pairs={{0,8},{4,12},{8,0},{12,4},{1,9},{5,13},{9,1},{13,5},{2,10},{6,14},... | collective-permute-start | bytes 393224 | tf_op jit(solution)/shard_map/ppermute | solution.py:25
  11.7 8.4 %collective-permute-start.4 = (bf16[128,512]{1,0:T(8,128)(2,1)S(1)}, bf16[128,512]{1,0:T(8,128)(2,1)S(1)}, u32[]{:S(2)}, u32[]{:S(2)}) collective-permute-start(bf16[128,512]{1,0:T(8,128)(2,1)S(1)} %shard_map.61.x_ref), channel_id=1, source_target_pairs={{0,4},{4,0},{8,12},{12,8},{1,5},{5,1},{9,13},{13,9},{2,6},{6,2},{1... | collective-permute-start | bytes 393224 | tf_op jit(solution)/shard_map/ppermute | solution.py:25
  17.6 5.2 %collective-permute-start.1 = (bf16[128,512]{1,0:T(8,128)(2,1)S(1)}, bf16[128,512]{1,0:T(8,128)(2,1)S(1)}, u32[]{:S(2)}, u32[]{:S(2)}) collective-permute-start(bf16[128,512]{1,0:T(8,128)(2,1)S(1)} %shard_map.54.x_ref), channel_id=1, source_target_pairs={{0,4},{4,0},{8,12},{12,8},{1,5},{5,1},{9,13},{13,9},{2,6},{6,2},{1... | collective-permute-start | bytes 393224 | tf_op jit(solution)/shard_map/ppermute | solution.py:25
  20.8 6.0 %collective-permute-start.5 = (bf16[128,512]{1,0:T(8,128)(2,1)S(1)}, bf16[128,512]{1,0:T(8,128)(2,1)S(1)}, u32[]{:S(2)}, u32[]{:S(2)}) collective-permute-start(bf16[128,512]{1,0:T(8,128)(2,1)S(1)} %shard_map.63.x_ref), channel_id=1, source_target_pairs={{0,2},{2,0},{1,3},{3,1},{4,6},{6,4},{5,7},{7,5},{8,10},{10,8},{9,1... | collective-permute-start | bytes 393224 | tf_op jit(solution)/shard_map/ppermute | solution.py:25
  23.6 5.5 %collective-permute-start.2 = (bf16[128,512]{1,0:T(8,128)(2,1)S(1)}, bf16[128,512]{1,0:T(8,128)(2,1)S(1)}, u32[]{:S(2)}, u32[]{:S(2)}) collective-permute-start(bf16[128,512]{1,0:T(8,128)(2,1)S(1)} %shard_map.56.x_ref), channel_id=1, source_target_pairs={{0,2},{2,0},{1,3},{3,1},{4,6},{6,4},{5,7},{7,5},{8,10},{10,8},{9,1... | collective-permute-start | bytes 393224 | tf_op jit(solution)/shard_map/ppermute | solution.py:25
where the time goes:
time: 31.1 us; the launch traced here: 30.9 us
  starting transfers between devices  11.5 us (37%)
  Pallas kernels  9.19 us (30%)
  waiting for transfers between devices  7.78 us (25%)
  local copies, waits for them, and re-layouts  2.3 us (7%)
    ppermute x6, starting transfers between devices, partner_2(): return lax.ppermute(value, axis, pairs)  11.5 us
    pallas_call x21, Pallas kernels, call(): pl.pallas_call(body, out_shape=outs, in_specs=in_specs or [vmem] * len(ar...  9.19 us
    ppermute x6, waiting for transfers between devices, partner_2(): return lax.ppermute(value, axis, pairs)  7.78 us
    unnamed x8, local copies, waits for them, and re-layouts  1.33 us
    slice x1, local copies, waits for them, and re-layouts, on_device(): pieces = [coeffs[:, :chunk]]  0.97 us
  transfers between devices with their start and end apart: 6, of which 6 were waited for; matrix products, arithmetic and copies ran while one was open for 0% of the time, Pallas kernels for 24%

commit v1 on v0

--- a/solution.py
+++ b/solution.py
@@ -16,7 +16,7 @@
 BF16 = jnp.bfloat16
 CHUNKS = 2
 LANES = 128
-EARLY = 4
+EARLY = 2
 
 
 def partner_2(value, axis, bit):
@@ -176,18 +176,38 @@
 
 
 def piece_body(begin, x_ref, *refs):
-    out_ref, sem = refs[-2:]
-    copy = pltpu.make_async_copy(x_ref.at[:, pl.ds(begin, out_ref.shape[1])], out_ref, sem)
-    copy.start()
-    copy.wait()
-
-
-def own_body(index, raw, x_ref, table_ref, w_ref, out_ref, flat_ref, mod_ref):
-    if raw:
+    out_ref, flat_ref = refs[-2:]
+    _, _, boxes_u, boxes_v, _ = x_ref.shape
+    boxes = boxes_u * boxes_v
+    ill = out_ref.shape[0] // (2 * boxes)
+    half = boxes * ill
+    for part in range(2):
+        for i in range(ill):
+            for u in range(boxes_u):
+                piece = x_ref[part, begin + i, u].astype(F32)
+                place = pl.ds(part * half + i * boxes + u * boxes_v, boxes_v)
+                for t in range(flat_ref.shape[0]):
+                    flat_ref[t, place] = piece[:, t * LANES : (t + 1) * LANES]
+        for box in range(boxes):
+            value = strided(flat_ref, part * half + box, ill, boxes)
+            out_ref[part * half + box * ill : part * half + (box + 1) * ill] = value.astype(BF16)
+
+
+def own_body(index, x_ref, table_ref, w_ref, out_ref, flat_ref, mod_ref):
+    if index is None:
+        out_ref[...] = dot(x_ref[...], w_ref[...])
+    else:
+        receive(x_ref, table_ref, index, flat_ref, mod_ref)
+        out_ref[...] = dot(mod_ref[...], w_ref[...])
+
+
+def receive(x_ref, table_ref, index, flat_ref, mod_ref):
+    if len(x_ref.shape) == 5:
         modulate_raw(x_ref, table_ref, index, flat_ref, mod_ref)
-        out_ref[...] = dot(mod_ref[...], w_ref[...])
     else:
-        out_ref[...] = dot(x_ref[...], w_ref[...])
+        boxes = table_ref.shape[2]
+        ill = x_ref.shape[0] // (2 * boxes)
+        modulate(x_ref, table_ref, index, mod_ref, boxes, ill, straight(boxes, ill))
 
 
 def rest_body(shape, partner_index, pairs, send_index, begin, done, *refs):
@@ -212,7 +232,7 @@
     if partner_index is None:
         got = got_ref[...]
     else:
-        modulate_raw(got_ref, table_ref, partner_index, flat_ref, mod_ref)
+        receive(got_ref, table_ref, partner_index, flat_ref, mod_ref)
         got = mod_ref[...]
     state_ref[...] = part_ref[...] + dot(got, w_ref[...])
     for number, (index, operator, bit) in enumerate(pairs):
@@ -232,13 +252,19 @@
                 for box in range(boxes):
                     if box >> box_bit & 1 == side:
                         start = place(part, box).start - side * half
-                        state_ref[straight(boxes, ill)(part, box)] = result[start : start + ill]
+                        value = result[start : start + ill]
+                        if send_index is None and number + 1 == len(pairs):
+                            for t in range(flat_ref.shape[0]):
+                                lanes = slice(t * LANES, (t + 1) * LANES)
+                                flat_ref[t, pl.ds(part * half + box, ill, stride=boxes)] = value[:, lanes]
+                        else:
+                            state_ref[straight(boxes, ill)(part, box)] = value
     if send_index is not None:
         modulate(state_ref, table_ref, send_index, out_ref, boxes, ill, straight(boxes, ill))
         return
     tiles = flat_ref.shape[0]
     for part in range(2):
-        for box in range(boxes):
+        for box in range(0 if pairs else boxes):
             value = state_ref[straight(boxes, ill)(part, box)]
             for t in range(tiles):
                 flat_ref[t, pl.ds(part * half + box, ill, stride=boxes)] = value[:, t * LANES : (t + 1) * LANES]
@@ -290,14 +316,13 @@
     def piece(begin, after):
         return call(
             functools.partial(piece_body, begin),
-            jax.ShapeDtypeStruct(piece_shape, BF16),
-            [pltpu.SemaphoreType.DMA],
+            jax.ShapeDtypeStruct((rows, coef_count), BF16),
+            [pltpu.VMEM((coef_count // LANES, rows, LANES), F32)],
             1000,
             rows * coef_count * 4,
             coeffs,
             *after,
-            in_specs=[anywhere] * (1 + len(after)),
-            limit=6 * 1024 * 1024,
+            in_specs=[vmem] + [anywhere] * len(after),
         )
 
     pieces = [coeffs[:, :chunk]]
@@ -345,7 +370,7 @@
     def own_part(number, current):
         index = swaps[number]
         return call(
-            functools.partial(own_body, index, number == 0),
+            functools.partial(own_body, index if number == 0 else None),
             jax.ShapeDtypeStruct((rows, coef_count), F32),
             [pltpu.VMEM((coef_count // LANES, rows, LANES), F32), pltpu.VMEM((rows, coef_count), BF16)],
             product_flops,

time: 31.1 us -> 30.9 us (level)
  waiting for transfers between devices: 7.78 us -> 7.38 us
    ppermute x6, waiting for transfers between devices: 7.78 us -> 7.38 us  [partner_2(): return lax.ppermute(value, axis, pairs)]
where the time goes in v1:
time: 30.9 us; the launch traced here: 30.7 us
  starting transfers between devices  11.6 us (38%)
  Pallas kernels  9.09 us (29%)
  waiting for transfers between devices  7.38 us (24%)
  local copies, waits for them, and re-layouts  2.47 us (8%)
    ppermute x6, starting transfers between devices, partner_2(): return lax.ppermute(value, axis, pairs)  11.6 us
    pallas_call x21, Pallas kernels, call(): pl.pallas_call(body, out_shape=outs, in_specs=in_specs or [vmem] * len(ar...  9.09 us
    ppermute x6, waiting for transfers between devices, partner_2(): return lax.ppermute(value, axis, pairs)  7.38 us
    unnamed x8, local copies, waits for them, and re-layouts  1.5 us
    slice x1, local copies, waits for them, and re-layouts, on_device(): pieces = [coeffs[:, :chunk]]  0.97 us
  transfers between devices with their start and end apart: 6, of which 6 were waited for; matrix products, arithmetic and copies ran while one was open for 0% of the time, Pallas kernels for 24%

profile of v1, /device:TPU:0, one launch (start us, length us, event | category | flops | bytes accessed | tf_op | source)
XLA Modules:
  0.0 30.7 jit_solution(2985219060590603719)
XLA Ops:
  0.0 1.0 %slice.3.x_ref = bf16[2,8,2,4,512]{4,3,2,1,0:T(4,128)(2,1)S(1)} slice(bf16[2,16,2,4,512]{4,3,2,1,0:T(4,128)(2,1)} %x_ref.1), slice={[0:2], [0:8], [0:2], [0:4], [0:512]} | slice | bytes 262144 | tf_op jit(solution)/shard_map/slice | solution.py:328
  1.0 4.1 %collective-permute-start.3 = (bf16[2,8,2,4,512]{4,3,2,1,0:T(4,128)(2,1)S(1)}, bf16[2,8,2,4,512]{4,3,2,1,0:T(4,128)(2,1)S(1)}, u32[]{:S(2)}, u32[]{:S(2)}) collective-permute-start(bf16[2,8,2,4,512]{4,3,2,1,0:T(4,128)(2,1)S(1)} %slice.3.x_ref), channel_id=1, source_target_pairs={{0,8},{4,12},{8,0},{12,4},{1,9},{5,13},{9,1},{13,5},{2,10},{6,14},... | collective-permute-start | bytes 393224 | tf_op jit(solution)/shard_map/ppermute | solution.py:25
  5.1 1.0 %copy-done.1 = f32[2,3,2,2,3,8,8]{6,5,4,3,2,1,0:T(8,128)S(1)} copy-done((f32[2,3,2,2,3,8,8]{6,5,4,3,2,1,0:T(8,128)S(1)}, f32[2,3,2,2,3,8,8]{6,5,4,3,2,1,0:T(8,128)}, u32[]{:S(2)}) %copy-start.1) | copy-done | bytes 18456
  6.1 0.7 %shard_map.47.spread_ref = f32[3,192,512]{2,1,0:T(8,128)S(1)} custom-call(f32[24,3,8,8]{3,2,1,0:T(8,128)S(1)} %bitcast.2), custom_call_target="tpu_custom_call" | custom-call | flops 2000000 | bytes 1000000 | tf_op jit(solution)/shard_map/pallas_call | solution.py:287
  6.8 0.3 shard_map.46.refs_0_.table_ref.refs_2_
  7.5 0.5 %copy-done = bf16[2,16,2,4,512]{4,3,2,1,0:T(4,128)(2,1)S(1)} copy-done((bf16[2,16,2,4,512]{4,3,2,1,0:T(4,128)(2,1)S(1)}, bf16[2,16,2,4,512]{4,3,2,1,0:T(4,128)(2,1)}, u32[]{:S(2)}) %copy-start) | copy-done | bytes 262168
  8.2 0.3 shard_map.60.refs_0_
  8.5 3.2 %collective-permute-done.3.refs_1_ = bf16[2,8,2,4,512]{4,3,2,1,0:T(4,128)(2,1)S(1)} collective-permute-done((bf16[2,8,2,4,512]{4,3,2,1,0:T(4,128)(2,1)S(1)}, bf16[2,8,2,4,512]{4,3,2,1,0:T(4,128)(2,1)S(1)}, u32[]{:S(2)}, u32[]{:S(2)}) %collective-permute-start.3) | collective-permute-done | bytes 131104 | tf_op jit(solution)/shard_map/ppermute | solution.py:25
  11.6 0.3 shard_map.61.x_ref
  11.9 3.5 %collective-permute-start.4 = (bf16[128,512]{1,0:T(8,128)(2,1)S(1)}, bf16[128,512]{1,0:T(8,128)(2,1)S(1)}, u32[]{:S(2)}, u32[]{:S(2)}) collective-permute-start(bf16[128,512]{1,0:T(8,128)(2,1)S(1)} %shard_map.61.x_ref), channel_id=1, source_target_pairs={{0,4},{4,0},{8,12},{12,8},{1,5},{5,1},{9,13},{13,9},{2,6},{6,2},{1... | collective-permute-start | bytes 393224 | tf_op jit(solution)/shard_map/ppermute | solution.py:25
  15.6 1.5 %collective-permute-done.refs_1_ = bf16[128,512]{1,0:T(8,128)(2,1)S(1)} collective-permute-done((bf16[128,512]{1,0:T(8,128)(2,1)S(1)}, bf16[128,512]{1,0:T(8,128)(2,1)S(1)}, u32[]{:S(2)}, u32[]{:S(2)}) %collective-permute-start) | collective-permute-done | bytes 131104 | tf_op jit(solution)/shard_map/ppermute | solution.py:25
  17.1 0.2 shard_map.52.x_ref
  17.4 0.7 %collective-permute-start.1 = (bf16[128,512]{1,0:T(8,128)(2,1)S(1)}, bf16[128,512]{1,0:T(8,128)(2,1)S(1)}, u32[]{:S(2)}, u32[]{:S(2)}) collective-permute-start(bf16[128,512]{1,0:T(8,128)(2,1)S(1)} %shard_map.52.x_ref), channel_id=1, source_target_pairs={{0,4},{4,0},{8,12},{12,8},{1,5},{5,1},{9,13},{13,9},{2,6},{6,2},{1... | collective-permute-start | bytes 393224 | tf_op jit(solution)/shard_map/ppermute | solution.py:25
  18.1 0.4 %shard_map.54 = (bf16[512,512]{1,0:T(8,128)(2,1)S(1)}, bf16[512,512]{1,0:T(8,128)(2,1)S(1)}, bf16[512,512]{1,0:T(8,128)(2,1)S(1)}, bf16[512,512]{1,0:T(8,128)(2,1)S(1)}) custom-call(f32[3,192,512]{2,1,0:T(8,128)S(1)} %shard_map.47.spread_ref), custom_call_target="tpu_custom_call" | custom-call | flops 80000000 | bytes 2097152 | tf_op jit(solution)/shard_map/pallas_call | solution.py:287
  18.7 1.2 %collective-permute-done.4.refs_1_ = bf16[128,512]{1,0:T(8,128)(2,1)S(1)} collective-permute-done((bf16[128,512]{1,0:T(8,128)(2,1)S(1)}, bf16[128,512]{1,0:T(8,128)(2,1)S(1)}, u32[]{:S(2)}, u32[]{:S(2)}) %collective-permute-start.4) | collective-permute-done | bytes 131104 | tf_op jit(solution)/shard_map/ppermute | solution.py:25
  19.9 0.7 %shard_map.63.x_ref = bf16[128,512]{1,0:T(8,128)(2,1)S(1)} custom-call(f32[128,512]{1,0:T(8,128)S(1)} %shard_map.62.refs_0_, bf16[128,512]{1,0:T(8,128)(2,1)S(1)} %collective-permute-done.4.refs_1_, f32[7,2,8,512]{3,2,1,0:T(8,128)S(1)} %shard_map.46.refs_0_.table_ref.refs_2_, bf16[512,512]{1,0:T(8,128)(2,1)S(1)} %get-tuple-element.24.refs_2_.refs_3_, ...), custom_call_target="tpu_custom_call" | custom-call | flops 201326592 | bytes 3145728 | tf_op jit(solution)/shard_map/pallas_call | solution.py:287
  20.6 1.6 %collective-permute-start.5 = (bf16[128,512]{1,0:T(8,128)(2,1)S(1)}, bf16[128,512]{1,0:T(8,128)(2,1)S(1)}, u32[]{:S(2)}, u32[]{:S(2)}) collective-permute-start(bf16[128,512]{1,0:T(8,128)(2,1)S(1)} %shard_map.63.x_ref), channel_id=1, source_target_pairs={{0,2},{2,0},{1,3},{3,1},{4,6},{6,4},{5,7},{7,5},{8,10},{10,8},{9,1... | collective-permute-start | bytes 393224 | tf_op jit(solution)/shard_map/ppermute | solution.py:25
  22.6 0.7 %shard_map.55.x_ref = bf16[128,512]{1,0:T(8,128)(2,1)S(1)} custom-call(f32[128,512]{1,0:T(8,128)S(1)} %shard_map.53.refs_0_, bf16[128,512]{1,0:T(8,128)(2,1)S(1)} %collective-permute-done.1.refs_1_, f32[7,2,8,512]{3,2,1,0:T(8,128)S(1)} %shard_map.46.refs_0_.table_ref.refs_2_, bf16[512,512]{1,0:T(8,128)(2,1)S(1)} %get-tuple-element.24.refs_2_.refs_3_, ...), custom_call_target="tpu_custom_call" | custom-call | flops 201326592 | bytes 3145728 | tf_op jit(solution)/shard_map/pallas_call | solution.py:287
  23.4 1.6 %collective-permute-start.2 = (bf16[128,512]{1,0:T(8,128)(2,1)S(1)}, bf16[128,512]{1,0:T(8,128)(2,1)S(1)}, u32[]{:S(2)}, u32[]{:S(2)}) collective-permute-start(bf16[128,512]{1,0:T(8,128)(2,1)S(1)} %shard_map.55.x_ref), channel_id=1, source_target_pairs={{0,2},{2,0},{1,3},{3,1},{4,6},{6,4},{5,7},{7,5},{8,10},{10,8},{9,1... | collective-permute-start | bytes 393224 | tf_op jit(solution)/shard_map/ppermute | solution.py:25
  25.2 0.4 %shard_map.59 = (bf16[512,512]{1,0:T(8,128)(2,1)S(1)}, bf16[512,512]{1,0:T(8,128)(2,1)S(1)}, bf16[512,512]{1,0:T(8,128)(2,1)S(1)}, bf16[512,512]{1,0:T(8,128)(2,1)S(1)}) custom-call(f32[3,192,512]{2,1,0:T(8,128)S(1)} %shard_map.47.spread_ref), custom_call_target="tpu_custom_call" | custom-call | flops 80000000 | bytes 2097152 | tf_op jit(solution)/shard_map/pallas_call | solution.py:287
  25.5 0.4 %shard_map.58 = (bf16[512,512]{1,0:T(8,128)(2,1)S(1)}, bf16[512,512]{1,0:T(8,128)(2,1)S(1)}, bf16[512,512]{1,0:T(8,128)(2,1)S(1)}, bf16[512,512]{1,0:T(8,128)(2,1)S(1)}) custom-call(f32[3,192,512]{2,1,0:T(8,128)S(1)} %shard_map.47.spread_ref), custom_call_target="tpu_custom_call" | custom-call | flops 80000000 | bytes 2097152 | tf_op jit(solution)/shard_map/pallas_call | solution.py:287
  26.6 1.2 %shard_map.65.refs_12_ = bf16[2,8,2,4,512]{4,3,2,1,0:T(4,128)(2,1)S(1)} custom-call(f32[128,512]{1,0:T(8,128)S(1)} %shard_map.64.refs_0_, bf16[128,512]{1,0:T(8,128)(2,1)S(1)} %collective-permute-done.5.refs_1_, f32[7,2,8,512]{3,2,1,0:T(8,128)S(1)} %shard_map.46.refs_0_.table_ref.refs_2_, bf16[512,512]{1,0:T(8,128)(2,1)S(1)} %get-tuple-element.32.refs_3_, ...), custom_call_target="tpu_custom_call" | custom-call | flops 335544320 | bytes 5242880 | tf_op jit(solution)/shard_map/pallas_call | solution.py:287
  27.8 1.1 %collective-permute-done.2.refs_1_ = bf16[128,512]{1,0:T(8,128)(2,1)S(1)} collective-permute-done((bf16[128,512]{1,0:T(8,128)(2,1)S(1)}, bf16[128,512]{1,0:T(8,128)(2,1)S(1)}, u32[]{:S(2)}, u32[]{:S(2)}) %collective-permute-start.2) | collective-permute-done | bytes 131104 | tf_op jit(solution)/shard_map/ppermute | solution.py:25
  28.9 1.8 %shard_map.66 = bf16[2,16,2,4,512]{4,3,2,1,0:T(4,128)(2,1)} custom-call(f32[128,512]{1,0:T(8,128)S(1)} %shard_map.57.refs_0_, bf16[128,512]{1,0:T(8,128)(2,1)S(1)} %collective-permute-done.2.refs_1_, f32[7,2,8,512]{3,2,1,0:T(8,128)S(1)} %shard_map.46.refs_0_.table_ref.refs_2_, bf16[512,512]{1,0:T(8,128)(2,1)S(1)} %get-tuple-element.32.refs_3_, ...), custom_call_target="tpu_custom_call" | custom-call | flops 335544320 | bytes 5242880 | tf_op jit(solution)/shard_map/pallas_call | solution.py:287
  (18 shorter events, 2.3 us)
Async XLA Ops:
  0.0 6.7 %copy-start.3 = (s32[512]{0:T(512)S(1)}, s32[512]{0:T(512)}, u32[]{:S(2)}) copy-start(s32[512]{0:T(512)} %param.7) | copy-start | bytes 6148
  0.0 6.7 %copy-start.2 = (f32[2,2,4,512]{3,2,1,0:T(4,128)S(1)}, f32[2,2,4,512]{3,2,1,0:T(4,128)}, u32[]{:S(2)}) copy-start(f32[2,2,4,512]{3,2,1,0:T(4,128)} %reflection_ref.1) | copy-start | bytes 98308
  1.0 10.6 %collective-permute-start.3 = (bf16[2,8,2,4,512]{4,3,2,1,0:T(4,128)(2,1)S(1)}, bf16[2,8,2,4,512]{4,3,2,1,0:T(4,128)(2,1)S(1)}, u32[]{:S(2)}, u32[]{:S(2)}) collective-permute-start(bf16[2,8,2,4,512]{4,3,2,1,0:T(4,128)(2,1)S(1)} %slice.3.x_ref), channel_id=1, source_target_pairs={{0,8},{4,12},{8,0},{12,4},{1,9},{5,13},{9,1},{13,5},{2,10},{6,14},... | collective-permute-start | bytes 393224 | tf_op jit(solution)/shard_map/ppermute | solution.py:25
  5.1 1.0 %copy-start.1 = (f32[2,3,2,2,3,8,8]{6,5,4,3,2,1,0:T(8,128)S(1)}, f32[2,3,2,2,3,8,8]{6,5,4,3,2,1,0:T(8,128)}, u32[]{:S(2)}) copy-start(f32[2,3,2,2,3,8,8]{6,5,4,3,2,1,0:T(8,128)} %param.6) | copy-start | bytes 55300
  7.1 1.0 %copy-start = (bf16[2,16,2,4,512]{4,3,2,1,0:T(4,128)(2,1)S(1)}, bf16[2,16,2,4,512]{4,3,2,1,0:T(4,128)(2,1)}, u32[]{:S(2)}) copy-start(bf16[2,16,2,4,512]{4,3,2,1,0:T(4,128)(2,1)} %x_ref.1) | copy-start | bytes 786436
  8.1 9.0 %collective-permute-start = (bf16[128,512]{1,0:T(8,128)(2,1)S(1)}, bf16[128,512]{1,0:T(8,128)(2,1)S(1)}, u32[]{:S(2)}, u32[]{:S(2)}) collective-permute-start(bf16[128,512]{1,0:T(8,128)(2,1)S(1)} %shard_map.50.x_ref), channel_id=1, source_target_pairs={{0,8},{4,12},{8,0},{12,4},{1,9},{5,13},{9,1},{13,5},{2,10},{6,14},... | collective-permute-start | bytes 393224 | tf_op jit(solution)/shard_map/ppermute | solution.py:25
  11.9 8.0 %collective-permute-start.4 = (bf16[128,512]{1,0:T(8,128)(2,1)S(1)}, bf16[128,512]{1,0:T(8,128)(2,1)S(1)}, u32[]{:S(2)}, u32[]{:S(2)}) collective-permute-start(bf16[128,512]{1,0:T(8,128)(2,1)S(1)} %shard_map.61.x_ref), channel_id=1, source_target_pairs={{0,4},{4,0},{8,12},{12,8},{1,5},{5,1},{9,13},{13,9},{2,6},{6,2},{1... | collective-permute-start | bytes 393224 | tf_op jit(solution)/shard_map/ppermute | solution.py:25
  17.4 5.3 %collective-permute-start.1 = (bf16[128,512]{1,0:T(8,128)(2,1)S(1)}, bf16[128,512]{1,0:T(8,128)(2,1)S(1)}, u32[]{:S(2)}, u32[]{:S(2)}) collective-permute-start(bf16[128,512]{1,0:T(8,128)(2,1)S(1)} %shard_map.52.x_ref), channel_id=1, source_target_pairs={{0,4},{4,0},{8,12},{12,8},{1,5},{5,1},{9,13},{13,9},{2,6},{6,2},{1... | collective-permute-start | bytes 393224 | tf_op jit(solution)/shard_map/ppermute | solution.py:25
  20.6 6.0 %collective-permute-start.5 = (bf16[128,512]{1,0:T(8,128)(2,1)S(1)}, bf16[128,512]{1,0:T(8,128)(2,1)S(1)}, u32[]{:S(2)}, u32[]{:S(2)}) collective-permute-start(bf16[128,512]{1,0:T(8,128)(2,1)S(1)} %shard_map.63.x_ref), channel_id=1, source_target_pairs={{0,2},{2,0},{1,3},{3,1},{4,6},{6,4},{5,7},{7,5},{8,10},{10,8},{9,1... | collective-permute-start | bytes 393224 | tf_op jit(solution)/shard_map/ppermute | solution.py:25
  23.4 5.5 %collective-permute-start.2 = (bf16[128,512]{1,0:T(8,128)(2,1)S(1)}, bf16[128,512]{1,0:T(8,128)(2,1)S(1)}, u32[]{:S(2)}, u32[]{:S(2)}) collective-permute-start(bf16[128,512]{1,0:T(8,128)(2,1)S(1)} %shard_map.55.x_ref), channel_id=1, source_target_pairs={{0,2},{2,0},{1,3},{3,1},{4,6},{6,4},{5,7},{7,5},{8,10},{10,8},{9,1... | collective-permute-start | bytes 393224 | tf_op jit(solution)/shard_map/ppermute | solution.py:25
